TPU v7x, 32 devices: a whole 2x2x4 slice. The times are simulated.
32 devices in a mesh: dp: 8 (over y, x, core), tensor: 4 (over z).
Axes of the slice: x: 2, y: 2, z: 4, core: 2. Of those that a mesh axis runs over, the one named last changes fastest.
Arguments:
- hidden: bfloat16 [1024, 8192], P('dp')
- q_weight: float32 [8192, 4096], P(('dp', 'tensor')), may hold values from -0.0625 to 0.0625
- k_weight: float32 [8192, 1024], P(('dp', 'tensor')), may hold values from -0.0625 to 0.0625
- v_weight: float32 [8192, 1024], P(('dp', 'tensor')), may hold values from -0.0625 to 0.0625
- o_weight: float32 [8192, 4096], P(('dp', 'tensor')), may hold values from -0.09375 to 0.09375
- input_gain: float32 [8192], replicated, may hold values from 0.25 to 1.75
- post_gain: float32 [8192], replicated, may hold values from 0.25 to 1.75
- key_cache: bfloat16 [1024, 64, 8, 128], P('dp', None, 'tensor'), may hold values from -1000 to 1000
- value_cache: bfloat16 [1024, 64, 8, 128], P('dp', None, 'tensor'), may hold values from -6 to 6
- lengths: int32 [1024], P('dp'), may hold values from 1 to 64
Outputs:
- new_hidden: bfloat16 [1024, 8192], P('dp')
- normed: bfloat16 [1024, 8192], P('dp')
- fresh_token_keys: bfloat16 [1024, 8, 128], P('dp', 'tensor')
- new_values: bfloat16 [1024, 8, 128], P('dp', 'tensor')
All inputs are finite; a program needn't handle non-finite values.
Results may differ from a plain program's by a relative error of at most 0.012.
The roundings to bfloat16 on the way count: a program that leaves them out, or rounds other values in their place, can miss the bound.
Values may be sent and summed in bfloat16 or wider, within the bound.
A program may use at most 128 MiB of HBM per device.

v0:
```python
import math
import jax
import jax.numpy as jnp
from jax import lax
from jax.sharding import PartitionSpec as P

HEADS = 32
KV_HEADS = 8
HEAD_DIM = 128
epsilon = 1e-05
rope_base = 500000.0


def rms_gain(values, gain_vector):
    mean_square = jnp.mean(values * values, axis=-1, keepdims=True)
    return values * lax.rsqrt(mean_square + epsilon) * gain_vector


def rotate(values, positions):
    half_dim = values.shape[-1] // 2
    index_row = jnp.arange(half_dim, dtype=jnp.float32)
    frequency = jnp.exp(-math.log(rope_base) * index_row / half_dim)
    angle = positions.astype(jnp.float32)[:, None, None] * frequency[None, None, :]
    first_half = values[..., :half_dim]
    second_half = values[..., half_dim:]
    return jnp.concatenate(
        [
            first_half * jnp.cos(angle) - second_half * jnp.sin(angle),
            second_half * jnp.cos(angle) + first_half * jnp.sin(angle),
        ],
        axis=-1,
    )


def attend(query_b, fresh_token_keys, new_values, key_cache, value_cache, lengths):
    row_count, kv_count = (fresh_token_keys.shape[0], fresh_token_keys.shape[1])
    grouped_heads = query_b.reshape(row_count, kv_count, -1, HEAD_DIM)
    reciprocal_root = 1.0 / math.sqrt(HEAD_DIM)
    scores = (
        jnp.einsum("bkgd,blkd->bkgl", grouped_heads, key_cache, preferred_element_type=jnp.float32)
        * reciprocal_root
    )
    self_token_score = (
        jnp.einsum(
            "lfxa,lfa->lfx", grouped_heads, fresh_token_keys, preferred_element_type=jnp.float32
        )
        * reciprocal_root
    )
    visible = jnp.arange(key_cache.shape[1], dtype=jnp.int32)[None, :] < lengths[:, None]
    scores = jnp.where(visible[:, None, None, :], scores, -jnp.inf)
    largest = jnp.maximum(jnp.max(scores, axis=-1), self_token_score)
    kept_exp = jnp.exp(scores - largest[..., None])
    own_exp = jnp.exp(self_token_score - largest)
    softmax_divisor = jnp.sum(kept_exp, axis=-1) + own_exp
    weights_kept = (kept_exp / softmax_divisor[..., None]).astype(jnp.bfloat16)
    own_weight = (own_exp / softmax_divisor).astype(jnp.bfloat16)
    attended = jnp.einsum(
        "bkgl,blkd->bkgd", weights_kept, value_cache, preferred_element_type=jnp.float32
    )
    attended = (
        attended
        + own_weight.astype(jnp.float32)[..., None] * new_values.astype(jnp.float32)[:, :, None, :]
    )
    return attended.reshape(row_count, -1).astype(jnp.bfloat16)


def shards(
    hidden,
    q_weight,
    k_weight,
    v_weight,
    o_weight,
    input_gain,
    post_gain,
    key_cache,
    value_cache,
    lengths,
):
    tensor_size = lax.axis_size("tensor")
    row_count = hidden.shape[0]
    heads_here = HEADS // tensor_size
    kv_here = KV_HEADS // tensor_size
    w_query, w_key, value_matrix, w_out = (
        lax.all_to_all(
            q_weight.astype(jnp.bfloat16), "tensor", split_axis=1, concat_axis=0, tiled=True
        ),
        lax.all_to_all(
            k_weight.astype(jnp.bfloat16), "tensor", split_axis=1, concat_axis=0, tiled=True
        ),
        lax.all_to_all(
            v_weight.astype(jnp.bfloat16), "tensor", split_axis=1, concat_axis=0, tiled=True
        ),
        lax.all_to_all(
            o_weight.astype(jnp.bfloat16), "tensor", split_axis=1, concat_axis=0, tiled=True
        ),
    )
    normal_in = rms_gain(hidden.astype(jnp.float32), input_gain).astype(jnp.bfloat16)
    portions = (
        lax.all_gather(w_query, "dp", axis=0, tiled=True),
        lax.all_gather(w_key, "dp", axis=0, tiled=True),
        lax.all_gather(value_matrix, "dp", axis=0, tiled=True),
    )
    query, key_part, value_part = tuple(
        (jnp.dot(normal_in, portion, preferred_element_type=jnp.float32) for portion in portions)
    )
    query_b = rotate(query.reshape(row_count, heads_here, HEAD_DIM), lengths).astype(jnp.bfloat16)
    fresh_token_keys = rotate(key_part.reshape(row_count, kv_here, HEAD_DIM), lengths).astype(
        jnp.bfloat16
    )
    new_values = value_part.reshape(row_count, kv_here, HEAD_DIM).astype(jnp.bfloat16)
    attended = attend(query_b, fresh_token_keys, new_values, key_cache, value_cache, lengths)
    partial_value = lax.dot_general(
        attended,
        lax.all_gather(w_out, "dp", axis=0, tiled=True),
        (((1,), (1,)), ((), ())),
        preferred_element_type=jnp.float32,
    )
    mixed = lax.psum(partial_value.astype(jnp.bfloat16), "tensor").astype(jnp.float32)
    residual = hidden.astype(jnp.float32) + mixed
    new_hidden = residual.astype(jnp.bfloat16)
    normed = rms_gain(residual, post_gain).astype(jnp.bfloat16)
    return (new_hidden, normed, fresh_token_keys, new_values)


def solution(mesh):
    in_specs = (
        P("dp", None),
        P(("dp", "tensor"), None),
        P(("dp", "tensor"), None),
        P(("dp", "tensor"), None),
        P(("dp", "tensor"), None),
        P(),
        P(),
        P("dp", None, "tensor", None),
        P("dp", None, "tensor", None),
        P("dp"),
    )
    out_specs = (P("dp", None), P("dp", None), P("dp", "tensor", None), P("dp", "tensor", None))
    return jax.shard_map(shards, mesh=mesh, in_specs=in_specs, out_specs=out_specs, check_vma=False)
```

profile of v0, /device:TPU:0, one launch (start us, length us, event | category | flops | bytes accessed | tf_op | source)
XLA Modules:
  0.0 400.4 jit_solution(6438174233000839104)
XLA Ops:
  7.2 1.5 copy.44
  8.7 20.6 %all_to_all.76 = bf16[256,4,256]{0,2,1:T(8,128)(2,1)S(1)} all-to-all(bf16[256,4,256]{0,2,1:T(8,128)(2,1)S(1)} %bitcast.47), channel_id=1, replica_groups=mesh['dp'=8,'tensor'=4] {'tensor'}, dimensions={1} | all-to-all | bytes 1048576 | tf_op jit(solution)/shard_map/all_to_all | solution.py:87
  29.4 1.0 copy.45
  30.7 16.6 %all_to_all.77 = bf16[256,4,256]{0,2,1:T(8,128)(2,1)S(1)} all-to-all(bf16[256,4,256]{0,2,1:T(8,128)(2,1)S(1)} %bitcast.48), channel_id=1, replica_groups=mesh['dp'=8,'tensor'=4] {'tensor'}, dimensions={1} | all-to-all | bytes 1048576 | tf_op jit(solution)/shard_map/all_to_all | solution.py:90
  47.3 1.0 copy.53
  48.4 4.0 copy.41
  52.3 50.3 %all_to_all.78 = bf16[256,4,1024]{0,2,1:T(8,128)(2,1)} all-to-all(bf16[256,4,1024]{0,2,1:T(8,128)(2,1)S(1)} %bitcast.40), channel_id=1, replica_groups=mesh['dp'=8,'tensor'=4] {'tensor'}, dimensions={1} | all-to-all | bytes 4194304 | tf_op jit(solution)/shard_map/all_to_all | solution.py:84
  102.6 3.9 copy.42
  106.6 3.8 copy.54
  110.4 50.5 %all_to_all.79 = bf16[256,4,1024]{0,2,1:T(8,128)(2,1)} all-to-all(bf16[256,4,1024]{0,2,1:T(8,128)(2,1)S(1)} %bitcast.41), channel_id=1, replica_groups=mesh['dp'=8,'tensor'=4] {'tensor'}, dimensions={1} | all-to-all | bytes 4194304 | tf_op jit(solution)/shard_map/all_to_all | solution.py:93
  160.9 4.1 %copy.55 = bf16[4,256,1024]{2,1,0:T(8,128)(2,1)} copy(bf16[4,256,1024]{1,2,0:T(8,128)(2,1)} %bitcast.45) | data formatting | bytes 4194304 | tf_op jit(solution)/shard_map/all_to_all | solution.py:93
  166.8 3.0 fusion.29
  170.0 2.9 convolution_convert_fusion.1
  174.2 22.8 %all-gather.5.cloned.1.call-done = bf16[8192,1024]{1,0:T(8,128)(2,1)} async-done(((bf16[1024,1024]{1,0:T(8,128)(2,1)}), bf16[8192,1024]{1,0:T(8,128)(2,1)}) %all-gather.5.cloned.1.call-update) | async-done | bytes 16777232 | tf_op jit(solution)/shard_map/all_gather | solution.py:99
  197.0 8.1 %convolution_bitcast_fusion = f32[16,8,8,128]{3,1,2,0:T(8,128)S(1)} fusion(bf16[8192,1024]{1,0:T(8,128)(2,1)} %all-gather.5.cloned.1.call-done, bf16[128,8192]{1,0:T(8,128)(2,1)S(1)} %copy-done, f32[8192]{0:T(1024)S(1)} %copy-done.6, f32[128]{0:T(128)S(1)} %add_rsqrt_fusion.1), kind=kOutput, calls=%fused_computation.16 | convolution fusion | flops 2151677952 | bytes 19431936 | tf_op jit(solution)/shard_map/dot_general | solution.py:104
  206.1 5.5 %fusion.32 = (f32[128,2,4]{2,1,0:T(2,128)S(1)}, f32[128,2,4,64]{3,2,1,0:T(4,128)S(1)}) fusion(bf16[128,64,2,128]{3,2,1,0:T(2,128)(2,1)} %param.17, bf16[128,2,4,64]{3,2,1,0:T(4,128)(2,1)S(1)} %bitcast.56, bf16[128,2,4,64]{3,2,1,0:T(4,128)(2,1)S(1)} %bitcast.54, pred[128,64]{1,0:T(8,128)(4,1)} %iota_compare_fusion), kind=kOutput, calls=%fused_computation.46 | convolution fusion | flops 17497088 | bytes 4730880 | tf_op jit(solution)/shard_map/bkgd,blkd->bkgl/dot_general | solution.py:40
  211.9 0.8 fusion.20
  213.1 3.5 fusion.14
  216.8 72.3 %all-gather.11.cloned.1.call-done = bf16[8192,1024]{1,0:T(8,128)(2,1)} async-done(((bf16[1024,1024]{1,0:T(8,128)(2,1)}), bf16[8192,1024]{1,0:T(8,128)(2,1)}) %all-gather.11.cloned.1.call-update) | async-done | bytes 16777232 | tf_op jit(solution)/shard_map/all_gather | solution.py:114
  289.1 12.9 %convolution_convert_fusion = bf16[128,8192]{1,0:T(8,128)(2,1)} fusion(bf16[128,1024]{1,0:T(8,128)(2,1)S(1)} %convert_element_type.83, bf16[8192,1024]{1,0:T(8,128)(2,1)} %all-gather.11.cloned.1.call-done), kind=kOutput, calls=%fused_computation | convolution fusion | flops 2148532224 | bytes 19136512 | tf_op jit(solution)/shard_map/dot_general | solution.py:112
  302.0 0.8 pad_maximum_fusion.1
  302.8 85.5 %all-reduce.2.cloned.1.call-done = bf16[128,8192]{1,0:T(8,128)(2,1)} async-done(((bf16[128,8192]{1,0:T(8,128)(2,1)}), bf16[128,8192]{1,0:T(8,128)(2,1)}) %all-reduce.2.cloned.1.call-update) | async-done | bytes 2097168 | tf_op jit(solution)/shard_map/psum | solution.py:118
  388.3 2.5 multiply_reduce_fusion
  390.8 3.0 multiply_convert_fusion
  (51 shorter events, 5.3 us)
Async XLA Ops:
  7.2 23.3 %copy-start.2 = (f32[256,1024]{1,0:T(8,128)S(1)}, f32[256,1024]{1,0:T(8,128)}, u32[]{:S(2)}) copy-start(f32[256,1024]{1,0:T(8,128)} %param.13) | copy-start | bytes 3145732
  7.2 159.7 %all-gather.7.cloned.1.call-start = ((), (), s32[]{:S(2)}) async-start(), calls=%async_computation.5 | async-start | bytes 4718592 | tf_op jit(solution)/shard_map/all_gather | solution.py:100
  30.4 139.6 %all-gather.9.cloned.1.call-start = ((), (), s32[]{:S(2)}) async-start(), calls=%async_computation.6 | async-start | bytes 4718592 | tf_op jit(solution)/shard_map/all_gather | solution.py:101
  48.3 148.7 %all-gather.5.cloned.1.call-start = ((), (), s32[]{:S(2)}) async-start(), calls=%async_computation.4 | async-start | bytes 18874368 | tf_op jit(solution)/shard_map/all_gather | solution.py:99
  106.6 182.5 %all-gather.11.cloned.1.call-start = ((), (), s32[]{:S(2)}) async-start(), calls=%async_computation.7 | async-start | bytes 18874368 | tf_op jit(solution)/shard_map/all_gather | solution.py:114
  160.9 4.4 %copy-start.5 = (s32[128]{0:T(128)S(1)}, s32[128]{0:T(128)}, u32[]{:S(2)}) copy-start(s32[128]{0:T(128)} %param.19) | copy-start | bytes 1540
  160.9 4.4 %copy-start = (bf16[128,8192]{1,0:T(8,128)(2,1)S(1)}, bf16[128,8192]{1,0:T(8,128)(2,1)}, u32[]{:S(2)}) copy-start(bf16[128,8192]{1,0:T(8,128)(2,1)} %param.10) | copy-start | bytes 6291460
  160.9 5.9 %copy-start.6 = (f32[8192]{0:T(1024)S(1)}, f32[8192]{0:T(1024)}, u32[]{:S(2)}) copy-start(f32[8192]{0:T(1024)} %param.15) | copy-start | bytes 98308
  165.0 223.3 %all-reduce.2.cloned.1.call-start = ((), (), s32[]{:S(2)}) async-start(), calls=%async_computation.8 | async-start | bytes 4194304 | tf_op jit(solution)/shard_map/psum | solution.py:118
  173.0 32.2 %copy-start.3 = (bf16[128,2,128]{2,1,0:T(2,128)(2,1)}, bf16[128,2,128]{2,1,0:T(2,128)(2,1)S(1)}, u32[]{:S(2)}) copy-start(bf16[128,2,128]{2,1,0:T(2,128)(2,1)S(1)} %convert_element_type.80) | copy-start | bytes 196612
  302.0 88.8 %copy-start.4 = (f32[8192]{0:T(1024)S(1)}, f32[8192]{0:T(1024)}, u32[]{:S(2)}) copy-start(f32[8192]{0:T(1024)} %param.16) | copy-start | bytes 98308
  388.3 2.5 copy-start.1
Sparse Core Ops, SparseCore 0:
  30.5 35.7 all-gather.6
  68.2 36.5 all-gather.8
  107.2 89.7 all-gather.4
  199.3 89.7 all-gather.10
  302.1 86.1 all-reduce.1
where the time goes:
time: 401 us; the launch traced here: 400 us
  waiting for transfers between devices  181 us (45%)
  blocking collectives  138 us (34%)
  matrix products  36.5 us (9%)
  local copies, waits for them, and re-layouts  20.6 us (5%)
  between operations  14 us (3%)
  other arithmetic  10.1 us (3%)
    psum x1, waiting for transfers between devices, shards(): lax.psum(partial_value.astype(jnp.bfloat16), 'tensor').astype(jnp.float32)  85.5 us
    all_gather x1, waiting for transfers between devices, shards(): lax.all_gather(w_out, 'dp', axis=0, tiled=True)  72.3 us
    all_to_all x1, blocking collectives, shards(): lax.all_to_all(o_weight.astype(jnp.bfloat16), 'tensor', split_axis=1, con...  50.5 us
    all_to_all x1, blocking collectives, shards(): lax.all_to_all(q_weight.astype(jnp.bfloat16), 'tensor', split_axis=1, con...  50.3 us
    all_gather x1, waiting for transfers between devices, shards(): lax.all_gather(w_query, 'dp', axis=0, tiled=True)  22.8 us
    all_to_all x1, blocking collectives, shards(): lax.all_to_all(k_weight.astype(jnp.bfloat16), 'tensor', split_axis=1, con...  20.6 us
    all_to_all x1, blocking collectives, shards(): lax.all_to_all(v_weight.astype(jnp.bfloat16), 'tensor', split_axis=1, con...  16.6 us
    dot_general x3, matrix products, shards(): jnp.dot(normal_in, portion, preferred_element_type=jnp.float32)  14.1 us
  transfers between devices with their start and end apart: 5, of which 3 were waited for; matrix products, arithmetic and copies ran while one was open for 12% of the time, Pallas kernels for 0%

commit v1 on v0

--- a/solution.py
+++ b/solution.py
@@ -81,8 +81,16 @@
     heads_here = HEADS // tensor_size
     kv_here = KV_HEADS // tensor_size
     w_query, w_key, value_matrix, w_out = (
-        lax.all_to_all(
-            q_weight.astype(jnp.bfloat16), "tensor", split_axis=1, concat_axis=0, tiled=True
+        jnp.concatenate(
+            lax.all_to_all(
+                jnp.stack(
+                    jnp.split(q_weight.astype(jnp.bfloat16), lax.axis_size("tensor"), axis=1)
+                ),
+                "tensor",
+                0,
+                0,
+            ),
+            axis=0,
         ),
         lax.all_to_all(
             k_weight.astype(jnp.bfloat16), "tensor", split_axis=1, concat_axis=0, tiled=True

time: 401 us -> 401 us (level)
  local copies, waits for them, and re-layouts: 20.6 us -> 12.9 us
  waiting for transfers between devices: 181 us -> 186 us
    all_gather x1, waiting for transfers between devices: 22.8 us -> 27.7 us  [shards(): lax.all_gather(w_query, 'dp', axis=0, tiled=True)]
    unnamed x19 -> x18, local copies, waits for them, and re-layouts: 9.56 us -> 5.65 us
  transfers between devices with their start and end apart: 5 -> 5, of which waited for: 3 -> 3; matrix products, arithmetic and copies ran while one was open for 12% -> 10% of each run, Pallas kernels for 0% -> 0%
where the time goes in v1:
time: 401 us; the launch traced here: 400 us
  waiting for transfers between devices  186 us (46%)
  blocking collectives  138 us (34%)
  matrix products  36.5 us (9%)
  between operations  14.1 us (4%)
  local copies, waits for them, and re-layouts  12.9 us (3%)
  other arithmetic  12.9 us (3%)
    psum x1, waiting for transfers between devices, shards(): lax.psum(partial_value.astype(jnp.bfloat16), 'tensor').astype(jnp.float32)  85.5 us
    all_gather x1, waiting for transfers between devices, shards(): lax.all_gather(w_out, 'dp', axis=0, tiled=True)  72.3 us
    all_to_all x1, blocking collectives, shards(): lax.all_to_all(jnp.stack(jnp.split(q_weight.astype(jnp.bfloat16), lax.axi...  50.5 us
    all_to_all x1, blocking collectives, shards(): lax.all_to_all(o_weight.astype(jnp.bfloat16), 'tensor', split_axis=1, con...  50.4 us
    all_gather x1, waiting for transfers between devices, shards(): lax.all_gather(w_query, 'dp', axis=0, tiled=True)  27.7 us
    all_to_all x1, blocking collectives, shards(): lax.all_to_all(k_weight.astype(jnp.bfloat16), 'tensor', split_axis=1, con...  20.6 us
    all_to_all x1, blocking collectives, shards(): lax.all_to_all(v_weight.astype(jnp.bfloat16), 'tensor', split_axis=1, con...  16.6 us
    dot_general x3, matrix products, shards(): jnp.dot(normal_in, portion, preferred_element_type=jnp.float32)  14 us
  transfers between devices with their start and end apart: 5, of which 3 were waited for; matrix products, arithmetic and copies ran while one was open for 10% of the time, Pallas kernels for 0%

profile of v1, /device:TPU:0, one launch (start us, length us, event | category | flops | bytes accessed | tf_op | source)
XLA Modules:
  0.0 400.4 jit_solution(10106508403615806058)
XLA Ops:
  7.2 1.5 copy.38
  8.7 20.6 %all_to_all.62 = bf16[256,4,256]{0,2,1:T(8,128)(2,1)S(1)} all-to-all(bf16[256,4,256]{0,2,1:T(8,128)(2,1)S(1)} %bitcast.51), channel_id=1, replica_groups=mesh['dp'=8,'tensor'=4] {'tensor'}, dimensions={1} | all-to-all | bytes 1048576 | tf_op jit(solution)/shard_map/all_to_all | solution.py:95
  29.4 1.0 copy.39
  30.7 16.6 %all_to_all.63 = bf16[256,4,256]{0,2,1:T(8,128)(2,1)S(1)} all-to-all(bf16[256,4,256]{0,2,1:T(8,128)(2,1)S(1)} %bitcast.52), channel_id=1, replica_groups=mesh['dp'=8,'tensor'=4] {'tensor'}, dimensions={1} | all-to-all | bytes 1048576 | tf_op jit(solution)/shard_map/all_to_all | solution.py:98
  47.3 1.0 copy.47
  48.3 2.5 convert_element_type.72
  51.3 50.5 %all_to_all.64 = bf16[4,256,1024]{2,1,0:T(8,128)(2,1)} all-to-all(bf16[4,256,1024]{2,1,0:T(8,128)(2,1)S(1)} %pad_maximum_fusion), channel_id=1, replica_groups=mesh['dp'=8,'tensor'=4] {'tensor'}, dimensions={0} | all-to-all | bytes 4194304 | tf_op jit(solution)/shard_map/all_to_all | solution.py:85
  101.8 3.8 copy.48
  105.7 50.4 %all_to_all.65 = bf16[256,4,1024]{0,2,1:T(8,128)(2,1)} all-to-all(bf16[256,4,1024]{0,2,1:T(8,128)(2,1)S(1)} %bitcast.46), channel_id=1, replica_groups=mesh['dp'=8,'tensor'=4] {'tensor'}, dimensions={1} | all-to-all | bytes 4194304 | tf_op jit(solution)/shard_map/all_to_all | solution.py:101
  156.1 4.1 %copy.49 = bf16[4,256,1024]{2,1,0:T(8,128)(2,1)} copy(bf16[4,256,1024]{1,2,0:T(8,128)(2,1)} %bitcast.49) | data formatting | bytes 4194304 | tf_op jit(solution)/shard_map/all_to_all | solution.py:101
  161.0 0.7 iota_compare_fusion
  162.0 2.9 fusion.29
  165.1 2.9 convolution_convert_fusion.1
  169.3 27.7 %all-gather.5.cloned.1.call-done = bf16[8192,1024]{1,0:T(8,128)(2,1)} async-done(((bf16[1024,1024]{1,0:T(8,128)(2,1)}), bf16[8192,1024]{1,0:T(8,128)(2,1)}) %all-gather.5.cloned.1.call-update) | async-done | bytes 16777232 | tf_op jit(solution)/shard_map/all_gather | solution.py:107
  197.0 8.1 %convolution_bitcast_fusion = f32[16,8,8,128]{3,1,2,0:T(8,128)S(1)} fusion(bf16[8192,1024]{1,0:T(8,128)(2,1)} %all-gather.5.cloned.1.call-done, bf16[128,8192]{1,0:T(8,128)(2,1)S(1)} %copy-done, f32[8192]{0:T(1024)S(1)} %copy-done.6, f32[128]{0:T(128)S(1)} %add_rsqrt_fusion.1), kind=kOutput, calls=%fused_computation.17 | convolution fusion | flops 2151677952 | bytes 19431936 | tf_op jit(solution)/shard_map/dot_general | solution.py:112
  206.1 5.5 %fusion.32 = (f32[128,2,4]{2,1,0:T(2,128)S(1)}, f32[128,2,4,64]{3,2,1,0:T(4,128)S(1)}) fusion(bf16[128,64,2,128]{3,2,1,0:T(2,128)(2,1)} %param.17, bf16[128,2,4,64]{3,2,1,0:T(4,128)(2,1)S(1)} %bitcast.60, bf16[128,2,4,64]{3,2,1,0:T(4,128)(2,1)S(1)} %bitcast.58, pred[128,64]{1,0:T(8,128)(4,1)} %iota_compare_fusion), kind=kOutput, calls=%fused_computation.51 | convolution fusion | flops 17497088 | bytes 4730880 | tf_op jit(solution)/shard_map/bkgd,blkd->bkgl/dot_general | solution.py:40
  211.9 0.8 fusion.20
  213.1 3.5 fusion.14
  216.8 72.3 %all-gather.11.cloned.1.call-done = bf16[8192,1024]{1,0:T(8,128)(2,1)} async-done(((bf16[1024,1024]{1,0:T(8,128)(2,1)}), bf16[8192,1024]{1,0:T(8,128)(2,1)}) %all-gather.11.cloned.1.call-update) | async-done | bytes 16777232 | tf_op jit(solution)/shard_map/all_gather | solution.py:122
  289.0 12.9 %convolution_convert_fusion = bf16[128,8192]{1,0:T(8,128)(2,1)} fusion(bf16[128,1024]{1,0:T(8,128)(2,1)S(1)} %convert_element_type.83, bf16[8192,1024]{1,0:T(8,128)(2,1)} %all-gather.11.cloned.1.call-done), kind=kOutput, calls=%fused_computation | convolution fusion | flops 2148532224 | bytes 19136512 | tf_op jit(solution)/shard_map/dot_general | solution.py:120
  302.0 0.8 pad_maximum_fusion.2
  302.8 85.5 %all-reduce.2.cloned.1.call-done = bf16[128,8192]{1,0:T(8,128)(2,1)} async-done(((bf16[128,8192]{1,0:T(8,128)(2,1)}), bf16[128,8192]{1,0:T(8,128)(2,1)}) %all-reduce.2.cloned.1.call-update) | async-done | bytes 2097168 | tf_op jit(solution)/shard_map/psum | solution.py:126
  388.3 2.5 multiply_reduce_fusion
  390.8 3.0 multiply_convert_fusion
  (52 shorter events, 5.1 us)
Async XLA Ops:
  7.2 23.3 %copy-start.2 = (f32[256,1024]{1,0:T(8,128)S(1)}, f32[256,1024]{1,0:T(8,128)}, u32[]{:S(2)}) copy-start(f32[256,1024]{1,0:T(8,128)} %param.13) | copy-start | bytes 3145732
  7.2 154.8 %all-gather.7.cloned.1.call-start = ((), (), s32[]{:S(2)}) async-start(), calls=%async_computation.5 | async-start | bytes 4718592 | tf_op jit(solution)/shard_map/all_gather | solution.py:108
  30.4 134.7 %all-gather.9.cloned.1.call-start = ((), (), s32[]{:S(2)}) async-start(), calls=%async_computation.6 | async-start | bytes 4718592 | tf_op jit(solution)/shard_map/all_gather | solution.py:109
  48.3 148.7 %all-gather.5.cloned.1.call-start = ((), (), s32[]{:S(2)}) async-start(), calls=%async_computation.4 | async-start | bytes 18874368 | tf_op jit(solution)/shard_map/all_gather | solution.py:107
  101.8 187.3 %all-gather.11.cloned.1.call-start = ((), (), s32[]{:S(2)}) async-start(), calls=%async_computation.7 | async-start | bytes 18874368 | tf_op jit(solution)/shard_map/all_gather | solution.py:122
  156.1 4.4 %copy-start.5 = (s32[128]{0:T(128)S(1)}, s32[128]{0:T(128)}, u32[]{:S(2)}) copy-start(s32[128]{0:T(128)} %param.19) | copy-start | bytes 1540
  156.1 4.4 %copy-start = (bf16[128,8192]{1,0:T(8,128)(2,1)S(1)}, bf16[128,8192]{1,0:T(8,128)(2,1)}, u32[]{:S(2)}) copy-start(bf16[128,8192]{1,0:T(8,128)(2,1)} %param.10) | copy-start | bytes 6291460
  156.1 5.9 %copy-start.6 = (f32[8192]{0:T(1024)S(1)}, f32[8192]{0:T(1024)}, u32[]{:S(2)}) copy-start(f32[8192]{0:T(1024)} %param.15) | copy-start | bytes 98308
  160.2 228.1 %all-reduce.2.cloned.1.call-start = ((), (), s32[]{:S(2)}) async-start(), calls=%async_computation.8 | async-start | bytes 4194304 | tf_op jit(solution)/shard_map/psum | solution.py:126
  168.1 37.1 %copy-start.3 = (bf16[128,2,128]{2,1,0:T(2,128)(2,1)}, bf16[128,2,128]{2,1,0:T(2,128)(2,1)S(1)}, u32[]{:S(2)}) copy-start(bf16[128,2,128]{2,1,0:T(2,128)(2,1)S(1)} %convert_element_type.80) | copy-start | bytes 196612
  302.0 88.8 %copy-start.4 = (f32[8192]{0:T(1024)S(1)}, f32[8192]{0:T(1024)}, u32[]{:S(2)}) copy-start(f32[8192]{0:T(1024)} %param.16) | copy-start | bytes 98308
  388.3 2.5 copy-start.1
Sparse Core Ops, SparseCore 0:
  30.5 35.6 all-gather.6
  68.7 36.5 all-gather.8
  107.2 89.7 all-gather.4
  199.3 89.7 all-gather.10
  302.1 86.1 all-reduce.1
